TPU v7x, 32 devices: a whole 2x2x4 slice. The times are simulated.
32 devices in a mesh: elem: 8 (over z, y), comp: 2 (over x), rep: 2 (over core).
Axes of the slice: x: 2, y: 2, z: 4, core: 2. Of those that a mesh axis runs over, the one named last changes fastest.
Arguments:
- velocity: float32 [3, 10, 10, 10, 2, 6144], P(None, 'comp', None, None, None, ('elem', 'rep')), may hold values from -6 to 6
- geometry: float32 [3, 3, 10, 10, 10, 2, 6144], P(None, None, 'comp', None, None, None, ('elem', 'rep')), may hold values from -40 to 40
- element_place: int32 [2, 6144], P('comp', ('elem', 'rep')), may hold values from 0 to 383, as said below
Outputs:
- pressure: float32 [10, 10, 10, 2, 6144], P(None, None, None, 'comp', ('elem', 'rep'))
Inputs may be any that keep to these rules, and one draw needn't show every extreme that they name: `element_place`: in each row and each aligned run of 384 entries of it, every value 0 to 383 appears once.
All inputs are finite; a program needn't handle non-finite values.
Results may differ from a plain program's by a relative error of at most 0.000071.
Values sent between devices are 32-bit elements; how exact they have to be, the bound alone decides.
A program may use at most 192 MiB of HBM per device.

v0:
```python
import jax
import jax.numpy as jnp
import numpy as np
from jax import lax
from jax.sharding import PartitionSpec as P

BLOCK_X = 6
BLOCK_Y = 8
BLOCK_Z = 8
GRID_Y = 4


exact_mode = lax.Precision.HIGHEST


def passed_along(x, axis, by):
    count = lax.axis_size(axis)
    pairs = [(i, i + by) for i in range(count) if 0 <= i + by < count]
    return lax.ppermute(x, axis, pairs)


def legendre_columns(points, degree):
    columns = [points * 0.0 + 1.0, points]
    for order in range(2, degree + 1):
        columns.append(
            ((2 * order - 1) * points * columns[order - 1] - (order - 1) * columns[order - 2])
            / order
        )
    return columns


def derivative_table(node_count):
    degree = node_count - 1
    points = np.cos(np.pi * np.arange(node_count) / degree)
    for sweep in range(100):
        columns = legendre_columns(points, degree)
        points = points - (points * columns[degree] - columns[degree - 1]) / (
            node_count * columns[degree]
        )
    points = np.sort(points)
    values = legendre_columns(points, degree)[degree]
    identity = np.eye(node_count)
    spacing = points[:, None] - points[None, :] + identity
    matrix = values[:, None] / (values[None, :] * spacing)
    matrix = np.where(identity > 0.5, 0.0, matrix)
    matrix[0, 0] = -degree * (degree + 1) / 4.0
    matrix[degree, degree] = degree * (degree + 1) / 4.0
    return matrix


def apply_transpose(deriv_table, flux_r, flux_s, flux_t):
    along_r = jnp.einsum("ia,i...->a...", deriv_table, flux_r, precision=exact_mode)
    along_s = jnp.einsum("ib,ai...->ab...", deriv_table, flux_s, precision=exact_mode)
    along_t = jnp.einsum("ic,abi...->abc...", deriv_table, flux_t, precision=exact_mode)
    return along_r + along_s + along_t


def local_pass(field, direction, block_grid):
    last_node = field.shape[0] - 1
    element_axis = 3 + direction
    extent = block_grid[direction]
    lower = lax.slice_in_dim(field, 0, 1, axis=direction)
    upper = lax.slice_in_dim(field, last_node, last_node + 1, axis=direction)
    zero_lower = jnp.zeros_like(lax.slice_in_dim(lower, 0, 1, axis=element_axis))
    add_upper = jnp.concatenate(
        [lax.slice_in_dim(lower, 1, extent, axis=element_axis), zero_lower], axis=element_axis
    )
    add_lower = jnp.concatenate(
        [zero_lower, lax.slice_in_dim(upper, 0, extent - 1, axis=element_axis)], axis=element_axis
    )
    node_iota = lax.broadcasted_iota(jnp.int32, field.shape, direction)
    field = field + jnp.where(node_iota == 0, add_lower, 0.0)
    return field + jnp.where(node_iota == last_node, add_upper, 0.0)


def node_keep(sign_code, last_node):
    if sign_code > 0:
        return slice(last_node, last_node + 1)
    if sign_code < 0:
        return slice(0, 1)
    return slice(None)


def element_keep(sign_code, extent):
    if sign_code > 0:
        return slice(extent - 1, extent)
    if sign_code < 0:
        return slice(0, 1)
    return slice(None)


def take_region(field, offset, block_grid):
    last_node = field.shape[0] - 1
    nodes_key = tuple((node_keep(component, last_node) for component in offset))
    elems_key = tuple(
        (element_keep(offset[dim_index], block_grid[dim_index]) for dim_index in range(3))
    )
    return field[nodes_key + elems_key]


def region_mask(shape, offset, block_grid):
    last_node = shape[0] - 1
    verdict = jnp.ones(shape, dtype=jnp.bool_)
    for dim_index in range(3):
        if offset[dim_index] != 0:
            node_target = last_node if offset[dim_index] > 0 else 0
            elem_target = block_grid[dim_index] - 1 if offset[dim_index] > 0 else 0
            verdict = jnp.logical_and(
                verdict, lax.broadcasted_iota(jnp.int32, shape, dim_index) == node_target
            )
            verdict = jnp.logical_and(
                verdict, lax.broadcasted_iota(jnp.int32, shape, 3 + dim_index) == elem_target
            )
    return verdict


def add_region(field, offset, values, block_grid):
    return field + jnp.where(region_mask(field.shape, offset, block_grid), values, 0.0)


def neighbor_offsets():
    listing = []
    for step_x in (-1, 0, 1):
        for step_y in (-1, 0, 1):
            for step_z in (-1, 0, 1):
                if step_x != 0 or step_y != 0 or step_z != 0:
                    listing.append((step_x, step_y, step_z))
    return listing


def inside(position, offset, extents):
    verdict = jnp.asarray(True)
    for dim_index in range(3):
        target = position[dim_index] + offset[dim_index]
        verdict = jnp.logical_and(
            verdict, jnp.logical_and(target >= 0, target < extents[dim_index])
        )
    return verdict


def body(velocity, geometry, element_place):
    comp_count = lax.axis_size("comp")
    half_nodes = velocity.shape[1]
    node_count = half_nodes * comp_count
    deriv_table = jnp.asarray(derivative_table(node_count), jnp.float32)
    fluxes = []
    for direction in range(3):
        fluxes.append(
            geometry[0, direction] * velocity[0]
            + geometry[1, direction] * velocity[1]
            + geometry[2, direction] * velocity[2]
        )
    flux_r, flux_s, flux_t = (
        lax.all_to_all(fluxes[0], "comp", split_axis=3, concat_axis=0, tiled=True),
        lax.all_to_all(fluxes[1], "comp", split_axis=3, concat_axis=0, tiled=True),
        lax.all_to_all(fluxes[2], "comp", split_axis=3, concat_axis=0, tiled=True),
    )
    owned_nodes = apply_transpose(deriv_table, flux_r, flux_s, flux_t)
    owned_nodes = owned_nodes[:, :, :, 0, :]
    places = element_place[0]
    sub_count = places.shape[0]
    place_matrix = (places[:, None] == jnp.arange(sub_count, dtype=jnp.int32)[None, :]).astype(
        jnp.float32
    )
    canonical = jnp.einsum("abci,ij->abcj", owned_nodes, place_matrix, precision=exact_mode)
    block_grid = (BLOCK_X, BLOCK_Y, BLOCK_Z)
    canonical = canonical.reshape((node_count, node_count, node_count) + block_grid)
    layers = comp_count * lax.axis_size("rep")
    stride_x = GRID_Y * layers
    strides = (stride_x, layers, 1)
    extents = (lax.axis_size(("elem", "comp", "rep")) // stride_x, GRID_Y, layers)
    device = lax.axis_index(("elem", "comp", "rep"))
    position = (device // stride_x, device // layers % GRID_Y, device % layers)
    local_only = canonical
    for direction in range(3):
        local_only = local_pass(local_only, direction, block_grid)
    assembled = local_only
    for offset in neighbor_offsets():
        opposite = tuple((-component for component in offset))
        outgoing = take_region(local_only, opposite, block_grid)
        shift_by = -sum((component * stride for component, stride in zip(offset, strides)))
        incoming = passed_along(outgoing.reshape(-1), ("elem", "comp", "rep"), shift_by)
        within = inside(position, offset, extents)
        payload = jnp.where(within, incoming, 0.0).reshape(outgoing.shape)
        assembled = add_region(assembled, offset, payload, block_grid)
    assembled = assembled.reshape(node_count, node_count, node_count, sub_count)
    result = jnp.einsum("abcj,ij->abci", assembled, place_matrix, precision=exact_mode)
    return result[:, :, :, None, :]


def solution(mesh):
    placed = (
        P(None, "comp", None, None, None, ("elem", "rep")),
        P(None, None, "comp", None, None, None, ("elem", "rep")),
        P("comp", ("elem", "rep")),
    )
    return jax.shard_map(
        body,
        mesh=mesh,
        in_specs=placed,
        out_specs=P(None, None, None, "comp", ("elem", "rep")),
        check_vma=False,
    )
```

profile of v0, /device:TPU:1, one launch (start us, length us, event | category | flops | bytes accessed | tf_op | source)
XLA Modules:
  0.0 408.6 jit_solution(2351560866955214997)
XLA Ops:
  3.9 7.8 %fusion.121 = (f32[1,1,5,10,10,2,384]{6,5,4,3,2,1,0:T(2,128)S(1)}, f32[1,1,5,10,10,2,384]{6,5,4,3,2,1,0:T(2,128)S(1)}, f32[1,1,5,10,10,2,384]{6,5,4,3,2,1,0:T(2,...) fusion(f32[3,3,5,10,10,2,384]{6,5,4,3,2,1,0:T(2,128)} %param.5), kind=kLoop, calls=%fused_computation.193 | loop fusion | bytes 27648000 | tf_op jit(solution)/shard_map/slice | solution.py:149
  11.7 4.5 %fusion.33 = (f32[5,10,10,2,384]{4,2,1,0,3:T(8,128)}, f32[5,10,10,2,384]{4,2,1,0,3:T(8,128)S(1)}, f32[5,10,10,2,384]{4,2,1,0,3:T(8,128)}) fusion(f32[1,5,10,10,2,384]{5,4,3,2,1,0:T(2,128)S(1)} %get-tuple-element.49, f32[1,1,5,10,10,2,384]{6,5,4,3,2,1,0:T(2,128)S(1)} %get-tuple-element.41, f32[1,5,10,10,2,384]{5,4,3,2,1,0:T(2,128)S(1)} %get-tuple-element.48, ...), kind=kLoop, calls=%fused_computation.61 | loop fusion | flops 5760000 | bytes 23040000 | tf_op jit(solution)/shard_map/add | solution.py:149
  16.2 32.4 %all_to_all.45 = f32[5,10,10,2,384]{4,2,1,0,3:T(8,128)} all-to-all(f32[5,10,10,2,384]{4,2,1,0,3:T(8,128)S(1)} %get-tuple-element.45), channel_id=1, replica_groups=mesh['elem'=8,'comp'=2,'rep'=2] {'comp'}, dimensions={3} | all-to-all | bytes 3072000 | tf_op jit(solution)/shard_map/all_to_all | solution.py:155
  57.1 23.1 %all-to-all-done.2 = f32[5,10,10,2,384]{4,2,1,0,3:T(8,128)S(1)} async-done(((f32[5,10,10,2,384]{4,2,1,0,3:T(8,128)}), f32[5,10,10,2,384]{4,2,1,0,3:T(8,128)S(1)}, u32[]{:S(2)}, u32[]{:S(2)}) %all-to-all-start.2) | async-done | bytes 1536032 | tf_op jit(solution)/shard_map/all_to_all | solution.py:156
  80.2 5.1 %all-to-all-start = ((f32[5,10,10,2,384]{4,2,1,0,3:T(8,128)}), f32[5,10,10,2,384]{4,2,1,0,3:T(8,128)}, u32[]{:S(2)}, u32[]{:S(2)}) async-start(f32[5,10,10,2,384]{4,2,1,0,3:T(8,128)} %get-tuple-element.44), calls=%async_computation | async-start | bytes 4915200 | tf_op jit(solution)/shard_map/all_to_all | solution.py:154
  94.9 17.1 %all-to-all-done = f32[5,10,10,2,384]{4,2,1,0,3:T(8,128)} async-done(((f32[5,10,10,2,384]{4,2,1,0,3:T(8,128)}), f32[5,10,10,2,384]{4,2,1,0,3:T(8,128)}, u32[]{:S(2)}, u32[]{:S(2)}) %all-to-all-start) | async-done | bytes 1536032 | tf_op jit(solution)/shard_map/all_to_all | solution.py:154
  112.0 7.6 %fusion.37 = f32[10,10,10,384]{3,0,2,1:T(8,128)S(1)} fusion(f32[10,10,384,10]{2,3,1,0:T(8,128)} %fusion.131, f32[10,10,384,10]{2,3,1,0:T(8,128)} %fusion.130, f32[10,10,1,1]{0,1,3,2:T(8,128)S(1)} %copy-done.11, f32[10,10,10,384]{3,2,1,0:T(8,128)} %bitcast.10), kind=kOutput, calls=%fused_computation.71 | convolution fusion | flops 46848000 | bytes 6144400 | tf_op jit(solution)/shard_map/ia,i...->a.../dot_general | solution.py:52
  122.7 15.3 %reshape.219 = f32[10,10,10,6,8,8]{5,4,3,2,1,0:T(8,128)} reshape(f32[10,10,10,384]{3,2,1,0:T(8,128)S(1)} %fusion.38) | data formatting | bytes 3072000 | tf_op jit(solution)/shard_map/reshape | solution.py:167
  149.3 20.9 %select_add_fusion.2 = f32[10,10,10,6,8,8]{5,4,3,2,1,0:T(8,128)} fusion(f32[10,10,10,6,8,8]{5,4,3,2,1,0:T(8,128)} %reshape.219, f32[10,10,6,8,8]{4,3,2,1,0:T(8,128)S(1)} %get-tuple-element.63, f32[10,10,6,8,8]{4,3,2,1,0:T(8,128)S(1)} %get-tuple-element.61, pred[10]{0:T(512)(128)(4,1)S(1)} %iota_compare_fusion.5, pred[10]{0:T(512)(128)(4,1)S(1)} %iota_compare_fusion.6), kind=kLoop, calls=%fused_computation.2 | loop fusion | flops 1536000 | bytes 3379220 | tf_op jit(solution)/shard_map/add | solution.py:73
  170.2 5.9 %fusion.120 = (f32[10,1,10,6,7,8]{5,4,3,2,1,0:T(8,128)}, f32[10,1,10,6,7,8]{5,4,3,2,1,0:T(8,128)}) fusion(f32[10,10,10,6,8,8]{5,4,3,2,1,0:T(8,128)} %select_add_fusion.2), kind=kLoop, calls=%fused_computation.192 | loop fusion | bytes 537600 | tf_op jit(solution)/shard_map/slice | solution.py:69
  176.1 6.9 %fusion.123 = (f32[10,1,10,6,8,8]{5,4,3,2,1,0:T(8,128)}, f32[10,10,6,8,8]{4,3,2,1,0:T(8,128)}, f32[10,10,6,8,8]{4,3,2,1,0:T(8,128)}, f32[10,1,10,6,8,8]{5,4,3,2,1,0:T(8,128)}) fusion(f32[10,1,10,6,7,8]{5,4,3,2,1,0:T(8,128)} %get-tuple-element.33, f32[10,1,10,6,7,8]{5,4,3,2,1,0:T(8,128)} %get-tuple-element.34), kind=kLoop, calls=%fused_computation.195 | loop fusion | bytes 883200 | tf_op jit(solution)/shard_map/concatenate | solution.py:68
  183.1 14.5 %select_add_fusion.1 = f32[10,10,10,6,8,8]{5,4,3,2,1,0:T(8,128)} fusion(f32[10,10,6,8,8]{4,3,2,1,0:T(8,128)} %get-tuple-element.64, f32[10,10,6,8,8]{4,3,2,1,0:T(8,128)} %get-tuple-element.51, pred[10]{0:T(512)(128)(4,1)S(1)} %iota_compare_fusion.5, pred[10]{0:T(512)(128)(4,1)S(1)} %iota_compare_fusion.6, f32[10,10,6,8,8]{4,3,2,1,0:T(8,128)S(1)} %get-tuple-element.63, ...), kind=kLoop, calls=%fused_computation.1 | loop fusion | flops 3072000 | bytes 3686420 | tf_op jit(solution)/shard_map/add | solution.py:73
  206.6 17.5 %select_add_fusion = f32[10,10,10,6,8,8]{5,4,3,2,1,0:T(8,128)} fusion(f32[10,10,6,8,8]{4,3,2,1,0:T(8,128)} %get-tuple-element.57, f32[10,10,6,8,8]{4,3,2,1,0:T(8,128)} %get-tuple-element.55, pred[10]{0:T(512)(128)(4,1)S(1)} %iota_compare_fusion.5, pred[10]{0:T(512)(128)(4,1)S(1)} %iota_compare_fusion.6, f32[10,10,6,8,8]{4,3,2,1,0:T(8,128)} %get-tuple-element.64, ...), kind=kLoop, calls=%fused_computation | loop fusion | flops 4608000 | bytes 3993620 | tf_op jit(solution)/shard_map/add | solution.py:73
  230.5 4.5 %slice_reduce_fusion.1 = (f32[10,10,6,8]{3,2,1,0:T(8,128)S(1)}, f32[10,10,6,8]{3,2,1,0:T(8,128)S(1)}) fusion(f32[10,10,10,6,8,8]{5,4,3,2,1,0:T(8,128)} %select_add_fusion), kind=kLoop, calls=%fused_computation.42 | loop fusion | bytes 76800 | tf_op jit(solution)/shard_map/slice | solution.py:98
  237.3 5.0 %slice_reduce_fusion.3 = (f32[10,10,6,8]{3,2,1,0:T(8,128)}, f32[10,10,6,8]{3,2,1,0:T(8,128)}) fusion(f32[10,10,10,6,8,8]{5,4,3,2,1,0:T(8,128)} %select_add_fusion), kind=kLoop, calls=%fused_computation.143 | loop fusion | bytes 76800 | tf_op jit(solution)/shard_map/slice | solution.py:98
  258.1 8.1 %collective-permute-start = (f32[1]{0:T(128)}, f32[1]{0:T(128)}, u32[]{:S(2)}, u32[]{:S(2)}) collective-permute-start(f32[1]{0:T(128)} %bitcast.39), channel_id=1, source_target_pairs={{0,21},{1,22},{2,23},{3,24},{4,25},{5,26},{6,27},{7,28},{8,29},{9,... | collective-permute-start | bytes 20 | tf_op jit(solution)/shard_map/ppermute | solution.py:19
  270.1 5.7 %collective-permute-start.8 = (f32[1]{0:T(128)}, f32[1]{0:T(128)}, u32[]{:S(2)}, u32[]{:S(2)}) collective-permute-start(f32[1]{0:T(128)} %bitcast.48), channel_id=1, source_target_pairs={{0,11},{1,12},{2,13},{3,14},{4,15},{5,16},{6,17},{7,18},{8,19},{9,... | collective-permute-start | bytes 20 | tf_op jit(solution)/shard_map/ppermute | solution.py:19
  289.4 8.4 %collective-permute-start.6 = (f32[1]{0:T(128)}, f32[1]{0:T(128)}, u32[]{:S(2)}, u32[]{:S(2)}) collective-permute-start(f32[1]{0:T(128)} %bitcast.45), channel_id=1, source_target_pairs={{0,13},{1,14},{2,15},{3,16},{4,17},{5,18},{6,19},{7,20},{8,21},{9,... | collective-permute-start | bytes 20 | tf_op jit(solution)/shard_map/ppermute | solution.py:19
  307.4 7.4 %collective-permute-start.9 = (f32[60]{0:T(128)S(1)}, f32[60]{0:T(128)S(1)}, u32[]{:S(2)}, u32[]{:S(2)}) collective-permute-start(f32[60]{0:T(128)S(1)} %reshape.229), channel_id=1, source_target_pairs={{0,5},{1,6},{2,7},{3,8},{4,9},{5,10},{6,11},{7,12},{8,13},{9,14},{... | collective-permute-start | bytes 728 | tf_op jit(solution)/shard_map/ppermute | solution.py:19
  322.4 6.4 %collective-permute-start.3 = (f32[80]{0:T(128)S(1)}, f32[80]{0:T(128)S(1)}, u32[]{:S(2)}, u32[]{:S(2)}) collective-permute-start(f32[80]{0:T(128)S(1)} %reshape.223), channel_id=1, source_target_pairs={{0,17},{1,18},{2,19},{3,20},{4,21},{5,22},{6,23},{7,24},{8,25},{9,... | collective-permute-start | bytes 968 | tf_op jit(solution)/shard_map/ppermute | solution.py:19
  338.7 5.8 %collective-permute-start.1 = (f32[80]{0:T(128)S(1)}, f32[80]{0:T(128)S(1)}, u32[]{:S(2)}, u32[]{:S(2)}) collective-permute-start(f32[80]{0:T(128)S(1)} %reshape.221), channel_id=1, source_target_pairs={{0,20},{1,21},{2,22},{3,23},{4,24},{5,25},{6,26},{7,27},{8,28},{9,... | collective-permute-start | bytes 968 | tf_op jit(solution)/shard_map/ppermute | solution.py:19
  351.5 4.0 collective-permute-start.10
  363.9 5.7 %collective-permute-start.4 = (f32[6400]{0:T(1024)}, f32[6400]{0:T(1024)}, u32[]{:S(2)}, u32[]{:S(2)}) collective-permute-start(f32[6400]{0:T(1024)} %reshape.224), channel_id=1, source_target_pairs={{0,16},{1,17},{2,18},{3,19},{4,20},{5,21},{6,22},{7,23},{8,24},{9,... | collective-permute-start | bytes 76808 | tf_op jit(solution)/shard_map/ppermute | solution.py:19
  391.9 13.5 %fusion.61 = f32[10,10,10,1,384]{4,2,1,0,3:T(8,128)S(1)} fusion(f32[10,10,10,384]{3,2,1,0:T(8,128)S(1)} %copy-done.3, f32[]{:T(128)} %bitcast.61, f32[10,384]{1,0:T(8,128)S(1)} %copy-done.17, f32[]{:T(128)} %bitcast.58, f32[10,384]{1,0:T(8,128)S(1)} %copy-done.21, f32[10,10,384]{2,1,0:T(8,128)} %broadcast_in_dim.546, f32[10,384]{1,0:T(8,128)S(1)} %copy-done.22, ...), kind=kOutput, calls=%fused_computation.94 | convolution fusion | flops 1811859456 | bytes 5103412 | tf_op jit(solution)/shard_map/abcj,ij->abci/dot_general | solution.py:187
  (270 shorter events, 148.5 us)
Async XLA Ops:
  48.7 31.5 %all-to-all-start.2 = ((f32[5,10,10,2,384]{4,2,1,0,3:T(8,128)}), f32[5,10,10,2,384]{4,2,1,0,3:T(8,128)S(1)}, u32[]{:S(2)}, u32[]{:S(2)}) async-start(f32[5,10,10,2,384]{4,2,1,0,3:T(8,128)} %get-tuple-element.46), calls=%async_computation.2 | async-start | bytes 4915200 | tf_op jit(solution)/shard_map/all_to_all | solution.py:156
  80.2 31.9 %all-to-all-start = ((f32[5,10,10,2,384]{4,2,1,0,3:T(8,128)}), f32[5,10,10,2,384]{4,2,1,0,3:T(8,128)}, u32[]{:S(2)}, u32[]{:S(2)}) async-start(f32[5,10,10,2,384]{4,2,1,0,3:T(8,128)} %get-tuple-element.44), calls=%async_computation | async-start | bytes 4915200 | tf_op jit(solution)/shard_map/all_to_all | solution.py:154
  258.1 29.5 %collective-permute-start = (f32[1]{0:T(128)}, f32[1]{0:T(128)}, u32[]{:S(2)}, u32[]{:S(2)}) collective-permute-start(f32[1]{0:T(128)} %bitcast.39), channel_id=1, source_target_pairs={{0,21},{1,22},{2,23},{3,24},{4,25},{5,26},{6,27},{7,28},{8,29},{9,... | collective-permute-start | bytes 20 | tf_op jit(solution)/shard_map/ppermute | solution.py:19
  266.2 23.3 %collective-permute-start.25 = (f32[1]{0:T(128)}, f32[1]{0:T(128)}, u32[]{:S(2)}, u32[]{:S(2)}) collective-permute-start(f32[1]{0:T(128)} %bitcast.60), channel_id=1, source_target_pairs={{21,0},{22,1},{23,2},{24,3},{25,4},{26,5},{27,6},{28,7},{29,8},{30... | collective-permute-start | bytes 20 | tf_op jit(solution)/shard_map/ppermute | solution.py:19
  267.5 31.0 %collective-permute-start.19 = (f32[1]{0:T(128)}, f32[1]{0:T(128)}, u32[]{:S(2)}, u32[]{:S(2)}) collective-permute-start(f32[1]{0:T(128)} %bitcast.54), channel_id=1, source_target_pairs={{13,0},{14,1},{15,2},{16,3},{17,4},{18,5},{19,6},{20,7},{21,8},{22... | collective-permute-start | bytes 20 | tf_op jit(solution)/shard_map/ppermute | solution.py:19
  268.8 32.3 %collective-permute-start.17 = (f32[1]{0:T(128)}, f32[1]{0:T(128)}, u32[]{:S(2)}, u32[]{:S(2)}) collective-permute-start(f32[1]{0:T(128)} %bitcast.51), channel_id=1, source_target_pairs={{11,0},{12,1},{13,2},{14,3},{15,4},{16,5},{17,6},{18,7},{19,8},{20... | collective-permute-start | bytes 20 | tf_op jit(solution)/shard_map/ppermute | solution.py:19
  270.1 33.5 %collective-permute-start.8 = (f32[1]{0:T(128)}, f32[1]{0:T(128)}, u32[]{:S(2)}, u32[]{:S(2)}) collective-permute-start(f32[1]{0:T(128)} %bitcast.48), channel_id=1, source_target_pairs={{0,11},{1,12},{2,13},{3,14},{4,15},{5,16},{6,17},{7,18},{8,19},{9,... | collective-permute-start | bytes 20 | tf_op jit(solution)/shard_map/ppermute | solution.py:19
  287.6 17.8 %collective-permute-start.23 = (f32[1]{0:T(128)}, f32[1]{0:T(128)}, u32[]{:S(2)}, u32[]{:S(2)}) collective-permute-start(f32[1]{0:T(128)} %bitcast.57), channel_id=1, source_target_pairs={{19,0},{20,1},{21,2},{22,3},{23,4},{24,5},{25,6},{26,7},{27,8},{28... | collective-permute-start | bytes 20 | tf_op jit(solution)/shard_map/ppermute | solution.py:19
  289.4 17.9 %collective-permute-start.6 = (f32[1]{0:T(128)}, f32[1]{0:T(128)}, u32[]{:S(2)}, u32[]{:S(2)}) collective-permute-start(f32[1]{0:T(128)} %bitcast.45), channel_id=1, source_target_pairs={{0,13},{1,14},{2,15},{3,16},{4,17},{5,18},{6,19},{7,20},{8,21},{9,... | collective-permute-start | bytes 20 | tf_op jit(solution)/shard_map/ppermute | solution.py:19
  301.1 18.7 %collective-permute-start.11 = (f32[60]{0:T(128)S(1)}, f32[60]{0:T(128)S(1)}, u32[]{:S(2)}, u32[]{:S(2)}) collective-permute-start(f32[60]{0:T(128)S(1)} %reshape.231), channel_id=1, source_target_pairs={{0,3},{1,4},{2,5},{3,6},{4,7},{5,8},{6,9},{7,10},{8,11},{9,12},{10... | collective-permute-start | bytes 728 | tf_op jit(solution)/shard_map/ppermute | solution.py:19
  303.5 17.5 %collective-permute-start.14 = (f32[60]{0:T(128)S(1)}, f32[60]{0:T(128)S(1)}, u32[]{:S(2)}, u32[]{:S(2)}) collective-permute-start(f32[60]{0:T(128)S(1)} %reshape.234), channel_id=1, source_target_pairs={{3,0},{4,1},{5,2},{6,3},{7,4},{8,5},{9,6},{10,7},{11,8},{12,9},{13... | collective-permute-start | bytes 728 | tf_op jit(solution)/shard_map/ppermute | solution.py:19
  305.4 17.0 %collective-permute-start.16 = (f32[60]{0:T(128)S(1)}, f32[60]{0:T(128)S(1)}, u32[]{:S(2)}, u32[]{:S(2)}) collective-permute-start(f32[60]{0:T(128)S(1)} %reshape.236), channel_id=1, source_target_pairs={{5,0},{6,1},{7,2},{8,3},{9,4},{10,5},{11,6},{12,7},{13,8},{14,9},{... | collective-permute-start | bytes 728 | tf_op jit(solution)/shard_map/ppermute | solution.py:19
  307.4 21.7 %collective-permute-start.9 = (f32[60]{0:T(128)S(1)}, f32[60]{0:T(128)S(1)}, u32[]{:S(2)}, u32[]{:S(2)}) collective-permute-start(f32[60]{0:T(128)S(1)} %reshape.229), channel_id=1, source_target_pairs={{0,5},{1,6},{2,7},{3,8},{4,9},{5,10},{6,11},{7,12},{8,13},{9,14},{... | collective-permute-start | bytes 728 | tf_op jit(solution)/shard_map/ppermute | solution.py:19
  315.4 20.6 %collective-permute-start.5 = (f32[80]{0:T(128)S(1)}, f32[80]{0:T(128)S(1)}, u32[]{:S(2)}, u32[]{:S(2)}) collective-permute-start(f32[80]{0:T(128)S(1)} %reshape.225), channel_id=1, source_target_pairs={{0,15},{1,16},{2,17},{3,18},{4,19},{5,20},{6,21},{7,22},{8,23},{9,... | collective-permute-start | bytes 968 | tf_op jit(solution)/shard_map/ppermute | solution.py:19
  319.7 17.6 %collective-permute-start.20 = (f32[80]{0:T(128)S(1)}, f32[80]{0:T(128)S(1)}, u32[]{:S(2)}, u32[]{:S(2)}) collective-permute-start(f32[80]{0:T(128)S(1)} %reshape.240), channel_id=1, source_target_pairs={{15,0},{16,1},{17,2},{18,3},{19,4},{20,5},{21,6},{22,7},{23,8},{24... | collective-permute-start | bytes 968 | tf_op jit(solution)/shard_map/ppermute | solution.py:19
  321.1 17.6 %collective-permute-start.22 = (f32[80]{0:T(128)S(1)}, f32[80]{0:T(128)S(1)}, u32[]{:S(2)}, u32[]{:S(2)}) collective-permute-start(f32[80]{0:T(128)S(1)} %reshape.242), channel_id=1, source_target_pairs={{17,0},{18,1},{19,2},{20,3},{21,4},{22,5},{23,6},{24,7},{25,8},{26... | collective-permute-start | bytes 968 | tf_op jit(solution)/shard_map/ppermute | solution.py:19
  322.4 22.1 %collective-permute-start.3 = (f32[80]{0:T(128)S(1)}, f32[80]{0:T(128)S(1)}, u32[]{:S(2)}, u32[]{:S(2)}) collective-permute-start(f32[80]{0:T(128)S(1)} %reshape.223), channel_id=1, source_target_pairs={{0,17},{1,18},{2,19},{3,20},{4,21},{5,22},{6,23},{7,24},{8,25},{9,... | collective-permute-start | bytes 968 | tf_op jit(solution)/shard_map/ppermute | solution.py:19
  329.1 17.4 %collective-permute-start.7 = (f32[80]{0:T(128)S(1)}, f32[80]{0:T(128)S(1)}, u32[]{:S(2)}, u32[]{:S(2)}) collective-permute-start(f32[80]{0:T(128)S(1)} %reshape.227), channel_id=1, source_target_pairs={{0,12},{1,13},{2,14},{3,15},{4,16},{5,17},{6,18},{7,19},{8,20},{9,... | collective-permute-start | bytes 968 | tf_op jit(solution)/shard_map/ppermute | solution.py:19
  344.5 19.4 %collective-permute-start.13 = (f32[4800]{0:T(1024)S(1)}, f32[4800]{0:T(1024)S(1)}, u32[]{:S(2)}, u32[]{:S(2)}) collective-permute-start(f32[4800]{0:T(1024)S(1)} %reshape.233), channel_id=1, source_target_pairs={{1,0},{2,1},{3,2},{4,3},{5,4},{6,5},{7,6},{8,7},{9,8},{10,9},{11,1... | collective-permute-start | bytes 57608 | tf_op jit(solution)/shard_map/ppermute | solution.py:19
  346.5 23.1 %collective-permute-start.12 = (f32[4800]{0:T(1024)S(1)}, f32[4800]{0:T(1024)S(1)}, u32[]{:S(2)}, u32[]{:S(2)}) collective-permute-start(f32[4800]{0:T(1024)S(1)} %reshape.232), channel_id=1, source_target_pairs={{0,1},{1,2},{2,3},{3,4},{4,5},{5,6},{6,7},{7,8},{8,9},{9,10},{10,1... | collective-permute-start | bytes 57608 | tf_op jit(solution)/shard_map/ppermute | solution.py:19
  350.2 19.5 %collective-permute-start.15 = (f32[4800]{0:T(1024)S(1)}, f32[4800]{0:T(1024)S(1)}, u32[]{:S(2)}, u32[]{:S(2)}) collective-permute-start(f32[4800]{0:T(1024)S(1)} %reshape.235), channel_id=1, source_target_pairs={{4,0},{5,1},{6,2},{7,3},{8,4},{9,5},{10,6},{11,7},{12,8},{13,9},{1... | collective-permute-start | bytes 57608 | tf_op jit(solution)/shard_map/ppermute | solution.py:19
  351.5 18.2 %collective-permute-start.10 = (f32[4800]{0:T(1024)S(1)}, f32[4800]{0:T(1024)S(1)}, u32[]{:S(2)}, u32[]{:S(2)}) collective-permute-start(f32[4800]{0:T(1024)S(1)} %reshape.230), channel_id=1, source_target_pairs={{0,4},{1,5},{2,6},{3,7},{4,8},{5,9},{6,10},{7,11},{8,12},{9,13},{1... | collective-permute-start | bytes 57608 | tf_op jit(solution)/shard_map/ppermute | solution.py:19
  355.5 28.2 %collective-permute-start.21 = (f32[6400]{0:T(1024)}, f32[6400]{0:T(1024)S(1)}, u32[]{:S(2)}, u32[]{:S(2)}) collective-permute-start(f32[6400]{0:T(1024)} %reshape.241), channel_id=1, source_target_pairs={{16,0},{17,1},{18,2},{19,3},{20,4},{21,5},{22,6},{23,7},{24,8},{25... | collective-permute-start | bytes 76808 | tf_op jit(solution)/shard_map/ppermute | solution.py:19
  363.9 19.5 %collective-permute-start.4 = (f32[6400]{0:T(1024)}, f32[6400]{0:T(1024)}, u32[]{:S(2)}, u32[]{:S(2)}) collective-permute-start(f32[6400]{0:T(1024)} %reshape.224), channel_id=1, source_target_pairs={{0,16},{1,17},{2,18},{3,19},{4,20},{5,21},{6,22},{7,23},{8,24},{9,... | collective-permute-start | bytes 76808 | tf_op jit(solution)/shard_map/ppermute | solution.py:19
  (49 other events, 774.7 us)
where the time goes:
time: 417 us; the launch traced here: 409 us
  local copies, waits for them, and re-layouts  148 us (35%)
  starting transfers between devices  92.2 us (22%)
  other arithmetic  57.6 us (14%)
  waiting for transfers between devices  40.2 us (10%)
  blocking collectives  32.4 us (8%)
  matrix products  31.4 us (8%)
  between operations  6.91 us (2%)
    ppermute x26, starting transfers between devices, passed_along(): return lax.ppermute(x, axis, pairs)  83.1 us
    add x3, other arithmetic, local_pass(): return field + jnp.where(node_iota == last_node, add_upper, 0.0)  52.9 us
    broadcast_in_dim x54, local copies, waits for them, and re-layouts, add_region(): jnp.where(region_mask(field.shape, offset, block_grid), values, 0.0)  32.5 us
    all_to_all x1, blocking collectives, body(): lax.all_to_all(fluxes[1], 'comp', split_axis=3, concat_axis=0, tiled=True)  32.4 us
    all_to_all x1, waiting for transfers between devices, body(): lax.all_to_all(fluxes[2], 'comp', split_axis=3, concat_axis=0, tiled=True)  23.1 us
    slice x7, local copies, waits for them, and re-layouts, take_region(): return field[nodes_key + elems_key]  18.2 us
    all_to_all x1, waiting for transfers between devices, body(): lax.all_to_all(fluxes[0], 'comp', split_axis=3, concat_axis=0, tiled=True)  17.1 us
    reshape x1, local copies, waits for them, and re-layouts, body(): canonical.reshape((node_count, node_count, node_count) + block_grid)  15.3 us
  transfers between devices with their start and end apart: 28, of which 2 were waited for; matrix products, arithmetic and copies ran while one was open for 12% of the time, Pallas kernels for 0%

commit v1 on v0

v1 whole, which is shorter than its diff:
```python
import functools

import jax
import jax.numpy as jnp
import numpy as np
from jax import lax
from jax.experimental import pallas as pl
from jax.experimental.pallas import tpu as pltpu
from jax.sharding import PartitionSpec as P

BLOCK = (6, 8, 8)
GRID_Y = 4
LANES = 128
MESH = pl.DeviceIdType.MESH
AWAY = -100000


def legendre_columns(points, degree):
    columns = [points * 0.0 + 1.0, points]
    for order in range(2, degree + 1):
        columns.append(
            ((2 * order - 1) * points * columns[order - 1] - (order - 1) * columns[order - 2])
            / order
        )
    return columns


def derivative_table(node_count):
    degree = node_count - 1
    points = np.cos(np.pi * np.arange(node_count) / degree)
    for sweep in range(100):
        columns = legendre_columns(points, degree)
        points = points - (points * columns[degree] - columns[degree - 1]) / (
            node_count * columns[degree]
        )
    points = np.sort(points)
    values = legendre_columns(points, degree)[degree]
    identity = np.eye(node_count)
    spacing = points[:, None] - points[None, :] + identity
    matrix = values[:, None] / (values[None, :] * spacing)
    matrix = np.where(identity > 0.5, 0.0, matrix)
    matrix[0, 0] = -degree * (degree + 1) / 4.0
    matrix[degree, degree] = degree * (degree + 1) / 4.0
    return matrix


def up(count, step):
    return -(-count // step) * step


class Rows:
    def __init__(self, n):
        self.n = n
        m = n - 2
        self.m = m
        self.c_low, self.c_high = 0, m
        self.b_low, self.b_high = 2 * m, 2 * m + n
        self.faces = up(2 * m + 2 * n, 8)
        self.plane = n * n
        self.plane_pad = up(n * n, 8)
        self.total = self.faces + m * m

    def nodes(self):
        n, m = self.n, self.m
        order = [None] * up(self.total, 8)
        for k in range(m):
            order[self.c_low + k] = (k + 1, 0)
            order[self.c_high + k] = (k + 1, n - 1)
        for k in range(n):
            order[self.b_low + k] = (0, k)
            order[self.b_high + k] = (n - 1, k)
        for b in range(m):
            for c in range(m):
                order[self.faces + b * m + c] = (b + 1, c + 1)
        return order


def plane_matrix(table, rows):
    n = rows.n
    order = rows.nodes()
    matrix = np.zeros((len(order), 2 * rows.plane_pad), np.float32)
    for r, node in enumerate(order):
        if node is not None:
            b, c = node
            for i in range(n):
                matrix[r, i * n + c] += table[i, b]
                matrix[r, rows.plane_pad + b * n + i] += table[i, c]
    top = jnp.asarray(matrix).astype(jnp.bfloat16)
    rest = (jnp.asarray(matrix) - top.astype(jnp.float32)).astype(jnp.bfloat16)
    return jnp.concatenate([top, rest], axis=0)


def halves(x):
    high = x.astype(jnp.bfloat16)
    low = (x - high.astype(jnp.float32)).astype(jnp.bfloat16)
    return high, low


def dot(a, b):
    return jnp.dot(a, b, preferred_element_type=jnp.float32)


def pair_dot(x, onehot):
    high, low = halves(x)
    return dot(high, onehot) + dot(low, onehot)


def kernel(sizes, place_ref, kmat_ref, vel_ref, geo_ref, out_ref,
           vel, geo, flux, stack, fbuf, sbuf, field, face, near, sel, selt, outb, inb,
           load_sem, fsend, frecv, ssend, srecv, isend, irecv, nsend, nrecv):
    n, half, tiles, table, rows, counts = sizes
    m = rows.m
    parts = tiles * 2
    comp_count, rep_count = counts
    e, h, r = lax.axis_index("elem"), lax.axis_index("comp"), lax.axis_index("rep")
    elem_count = lax.axis_size("elem")
    other = 1 - h
    layers = comp_count * rep_count
    device = e * layers + h * rep_count + r
    stride_x = GRID_Y * layers
    extents = (elem_count * layers // stride_x, GRID_Y, layers)
    strides = (stride_x, layers, 1)
    position = (device // stride_x, (device // layers) % GRID_Y, device % layers)

    def coords(target):
        return (target // layers, (target // rep_count) % comp_count, target % rep_count)

    def has(d, side):
        if side == 0:
            return position[d] > 0
        return position[d] < extents[d] - 1

    def neighbour(d, side):
        return coords(device + (strides[d] if side == 1 else -strides[d]))

    def plane_at(k):
        return h * (half - 1) + k * (1 - 2 * h)

    def load(k, what):
        i = plane_at(k)
        if what == 0:
            return pltpu.make_async_copy(vel_ref.at[:, i], vel.at[:, i], load_sem.at[0, k])
        if what == 1:
            return pltpu.make_async_copy(geo_ref.at[:, 0, i], geo.at[:, 0, i], load_sem.at[1, k])
        return pltpu.make_async_copy(
            geo_ref.at[:, pl.ds(1, 2), i], geo.at[:, pl.ds(1, 2), i], load_sem.at[2, k]
        )

    for k in range(half):
        load(k, 0).start()
        load(k, 1).start()
    for k in range(half):
        load(k, 2).start()

    barrier = pltpu.get_barrier_semaphore()
    pl.semaphore_signal(barrier, inc=1, device_id=(e, other, r), device_id_type=MESH)
    expected = jnp.int32(1)
    for d in range(3):
        for side in range(2):
            @pl.when(has(d, side))
            def _():
                pl.semaphore_signal(
                    barrier, inc=1, device_id=neighbour(d, side), device_id_type=MESH
                )
            expected = expected + has(d, side).astype(jnp.int32)
    pl.semaphore_wait(barrier, expected)

    peer = (e, other, r)

    def flux_copy(k, first):
        a = first * half + (first * (half - 1) + k * (1 - 2 * first))
        q = 1 - first
        return pltpu.make_async_remote_copy(
            src_ref=fbuf.at[q, a], dst_ref=fbuf.at[q, a], send_sem=fsend.at[k],
            recv_sem=frecv.at[k], device_id=peer, device_id_type=MESH)

    def face_copy(k, first):
        a = first * half + (first * (half - 1) + k * (1 - 2 * first))
        q = 1 - first
        ref = sbuf.at[q, a, :, pl.ds(0, rows.faces)]
        return pltpu.make_async_remote_copy(
            src_ref=ref, dst_ref=ref, send_sem=ssend.at[k],
            recv_sem=srecv.at[k], device_id=peer, device_id_type=MESH)

    def inner_copy(k, first):
        a = first * half + (first * (half - 1) + k * (1 - 2 * first))
        q = 1 - first
        ref = sbuf.at[q, a, :, pl.ds(rows.faces, m * m)]
        return pltpu.make_async_remote_copy(
            src_ref=ref, dst_ref=ref, send_sem=isend.at[k],
            recv_sem=irecv.at[k], device_id=peer, device_id_type=MESH)

    def weigh(i, j, slot):
        flux[slot] = (geo[0, j, i] * vel[0, i] + geo[1, j, i] * vel[1, i]
                      + geo[2, j, i] * vel[2, i])

    def first_flux(k, carry):
        i = plane_at(k)
        a = h * half + i
        load(k, 0).wait()
        load(k, 1).wait()
        weigh(i, 0, 0)
        for q in range(2):
            for t in range(tiles):
                fbuf[q, a, t, pl.ds(0, rows.plane), :] = flux[0, pl.ds(t * 2 + q, rows.plane, stride=parts), :]
        flux_copy(k, h).start()
        return carry

    lax.fori_loop(0, half, first_flux, 0)

    stack[...] = jnp.zeros_like(stack)

    def plane_terms(k, carry):
        i = plane_at(k)
        a = h * half + i
        load(k, 2).wait()
        weigh(i, 1, 0)
        weigh(i, 2, 1)
        tall = up(rows.total, 8)
        for q in range(2):
            for j in range(2):
                for t in range(tiles):
                    stack[q, pl.ds(j * rows.plane_pad, rows.plane), pl.ds(t * LANES, LANES)] = (
                        flux[j, pl.ds(t * 2 + q, rows.plane, stride=parts), :])
            high, low = halves(stack[q])
            both = dot(kmat_ref[...], high)
            term = both[:tall] + both[tall:] + dot(kmat_ref[pl.ds(0, tall)], low)
            for t in range(tiles):
                sbuf[q, a, t] = term[:, t * LANES:(t + 1) * LANES]
        face_copy(k, h).start()

        @pl.when(k == 0)
        def _():
            inner_copy(0, h).start()
        return carry

    lax.fori_loop(0, half, plane_terms, 0)
    for k in range(1, half):
        inner_copy(k, h).start()

    lanes = tiles * LANES
    row = place_ref[...]
    col = jnp.transpose(
        jnp.broadcast_to(row.astype(jnp.float32), (LANES, lanes))).astype(jnp.int32)[:, :1]
    bx, by, bz = BLOCK

    def keys(p):
        x, y, z = p // (by * bz), (p // bz) % by, p % bz
        at, on = (x, y, z), (p % (by * bz), x * bz + z, p // bz)
        result = []
        for d in range(3):
            jump = (by * bz, bz, 1)[d]
            low, high = at[d] == 0, at[d] == BLOCK[d] - 1
            result.append((
                (jnp.where(low, AWAY, p - jump), jnp.where(low, on[d], AWAY)),
                (jnp.where(high, AWAY, p + jump), jnp.where(high, on[d], AWAY)),
            ))
        return result

    col_keys, row_keys = keys(col), keys(row)
    lane_at = lax.broadcasted_iota(jnp.int32, (lanes, LANES), 1)
    sub_at = lax.broadcasted_iota(jnp.int32, (LANES, lanes), 0)

    def onehot(verdict):
        return jnp.where(verdict, 1.0, 0.0).astype(jnp.bfloat16)

    for d in range(3):
        for side in range(2):
            near[d, side] = onehot(col_keys[d][side][0] == row)
            sel[d, side] = onehot(col_keys[d][side][1] == lane_at)
            selt[d, side] = onehot(sub_at == row_keys[d][side][1])

    def arrive_flux(k, carry):
        flux_copy(k, other).wait_recv()
        return carry

    lax.fori_loop(0, half, arrive_flux, 0)

    def along_first(g, carry):
        at = pl.ds(pl.multiple_of(g * 8, 8), 8)
        for t in range(tiles):
            values = [fbuf[h, i, t, at, :] for i in range(n)]
            for a in range(n):
                total = values[0] * float(table[0, a])
                for i in range(1, n):
                    total = total + values[i] * float(table[i, a])
                field[a, t, at, :] = total
        return carry

    lax.fori_loop(0, rows.plane_pad // 8, along_first, 0)

    def arrive_faces(k, carry):
        face_copy(k, other).wait_recv()
        return carry

    lax.fori_loop(0, half, arrive_faces, 0)
    inner_copy(0, other).wait_recv()

    def add_faces(a, carry):
        for t in range(tiles):
            for start, count, at in (
                (rows.c_low, m, pl.ds(n, m, stride=n)),
                (rows.c_high, m, pl.ds(2 * n - 1, m, stride=n)),
                (rows.b_low, n, pl.ds(0, n)),
                (rows.b_high, n, pl.ds(n * (n - 1), n)),
            ):
                field[a, t, at, :] = field[a, t, at, :] + sbuf[h, a, t, pl.ds(start, count), :]
        return carry

    lax.fori_loop(0, n, add_faces, 0)

    def add_inner(a):
        for t in range(tiles):
            for b in range(m):
                at = pl.ds(n * (b + 1) + 1, m)
                field[a, t, at, :] = (
                    field[a, t, at, :] + sbuf[h, a, t, pl.ds(rows.faces + b * m, m), :])

    add_inner(0)
    add_inner(n - 1)

    def take(d, side):
        node = side * (n - 1)
        if d == 0:
            return
        def one(a, carry):
            for t in range(tiles):
                at = pl.ds(node * n, n) if d == 1 else pl.ds(node, n, stride=n)
                face[side, t, pl.ds(a * n, n), :] = field[a, t, at, :]
            return carry
        lax.fori_loop(0, n, one, 0)

    def give(d, side, values):
        node = side * (n - 1)
        for t in range(tiles):
            piece = values[:, t * LANES:(t + 1) * LANES]
            if d == 0:
                field[node, t] = piece
            else:
                face[side, t] = piece
        if d == 0:
            return
        def one(a, carry):
            for t in range(tiles):
                at = pl.ds(node * n, n) if d == 1 else pl.ds(node, n, stride=n)
                field[a, t, at, :] = face[side, t, pl.ds(a * n, n), :]
            return carry
        lax.fori_loop(0, n, one, 0)

    def whole(d, side):
        source = field.at[side * (n - 1)] if d == 0 else face.at[side]
        return jnp.concatenate([source[t] for t in range(tiles)], axis=1)

    def step_copy(d, side):
        return pltpu.make_async_remote_copy(
            src_ref=outb.at[d, side], dst_ref=inb.at[d, 1 - side],
            send_sem=nsend.at[d, side], recv_sem=nrecv.at[d, 1 - side],
            device_id=neighbour(d, side), device_id_type=MESH)

    def step_arrival(d, side):
        return pltpu.make_async_remote_copy(
            src_ref=outb.at[d, side], dst_ref=inb.at[d, side],
            send_sem=nsend.at[d, side], recv_sem=nrecv.at[d, side],
            device_id=neighbour(d, side), device_id_type=MESH)

    for d in range(3):
        for side in range(2):
            take(d, side)
        split = []
        for side in range(2):
            values = whole(d, side)
            high, low = halves(values)
            split.append((values, high, low))
            outb[d, side] = dot(high, sel[d, side]) + dot(low, sel[d, side])

            @pl.when(has(d, side))
            def _():
                step_copy(d, side).start()
        totals = []
        for side in range(2):
            _, high, low = split[1 - side]
            totals.append(
                split[side][0] + (dot(high, near[d, 1 - side]) + dot(low, near[d, 1 - side])))
        for side in range(2):
            @pl.when(has(d, side))
            def _():
                step_arrival(d, side).wait_recv()

            @pl.when(jnp.logical_not(has(d, side)))
            def _():
                inb[d, side] = jnp.zeros(inb.shape[2:], jnp.float32)
        for side in range(2):
            give(d, side, totals[side] + pair_dot(inb[d, side], selt[d, side]))

    def arrive_inner(k, carry):
        inner_copy(k, other).wait_recv()
        return carry

    lax.fori_loop(1, half, arrive_inner, 0)

    def inner_planes(a, carry):
        add_inner(a)
        return carry

    lax.fori_loop(1, n - 1, inner_planes, 0)

    def put(a, carry):
        for t in range(tiles):
            out_ref[a, pl.ds(t, rows.plane, stride=tiles), :] = field[a, t, pl.ds(0, rows.plane), :]
        return carry

    lax.fori_loop(0, n, put, 0)

    for k in range(half):
        flux_copy(k, h).wait_send()
        face_copy(k, h).wait_send()
        inner_copy(k, h).wait_send()
    for d in range(3):
        for side in range(2):
            @pl.when(has(d, side))
            def _():
                step_copy(d, side).wait_send()


def body(velocity, geometry, element_place):
    comp_count, rep_count = lax.axis_size("comp"), lax.axis_size("rep")
    half, n = velocity.shape[1], velocity.shape[2]
    elems = velocity.shape[-1]
    tiles = elems // LANES
    table = np.asarray(derivative_table(n), np.float32)
    rows = Rows(n)
    parts = tiles * 2

    def view(x):
        lead = x.shape[:-4]
        x = x.reshape(lead + (n * n, 2, tiles, LANES))
        x = jnp.swapaxes(x, -2, -3)
        return x.reshape(lead + (n * n * parts, LANES))

    tall = up(rows.total, 8)
    deep = rows.plane_pad
    long = n * n * parts
    f32, bf16 = jnp.float32, jnp.bfloat16
    dma = pltpu.SemaphoreType.DMA
    result = pl.pallas_call(
        functools.partial(kernel, (n, half, tiles, table, rows, (comp_count, rep_count))),
        out_shape=jax.ShapeDtypeStruct((n, n * n * tiles, LANES), f32),
        in_specs=[
            pl.BlockSpec(memory_space=pltpu.VMEM),
            pl.BlockSpec(memory_space=pltpu.VMEM),
            pl.BlockSpec(memory_space=pl.ANY),
            pl.BlockSpec(memory_space=pl.ANY),
        ],
        out_specs=pl.BlockSpec(memory_space=pltpu.VMEM),
        scratch_shapes=[
            pltpu.VMEM((3, half, long, LANES), f32),
            pltpu.VMEM((3, 3, half, long, LANES), f32),
            pltpu.VMEM((2, long, LANES), f32),
            pltpu.VMEM((2, 2 * deep, elems), f32),
            pltpu.VMEM((2, n, tiles, deep, LANES), f32),
            pltpu.VMEM((2, n, tiles, tall, LANES), f32),
            pltpu.VMEM((n, tiles, deep, LANES), f32),
            pltpu.VMEM((2, tiles, deep, LANES), f32),
            pltpu.VMEM((3, 2, elems, elems), bf16),
            pltpu.VMEM((3, 2, elems, LANES), bf16),
            pltpu.VMEM((3, 2, LANES, elems), bf16),
            pltpu.VMEM((3, 2, deep, LANES), f32),
            pltpu.VMEM((3, 2, deep, LANES), f32),
            dma((3, half)),
            dma((half,)), dma((half,)), dma((half,)), dma((half,)), dma((half,)), dma((half,)),
            dma((3, 2)), dma((3, 2)),
        ],
        compiler_params=pltpu.CompilerParams(
            collective_id=0, has_side_effects=True, vmem_limit_bytes=60 * 1024 * 1024
        ),
    )(element_place, plane_matrix(table, rows), view(velocity), view(geometry))
    return result.reshape(n, n, n, 1, elems)


def solution(mesh):
    placed = (
        P(None, "comp", None, None, None, ("elem", "rep")),
        P(None, None, "comp", None, None, None, ("elem", "rep")),
        P("comp", ("elem", "rep")),
    )
    return jax.shard_map(
        body,
        mesh=mesh,
        in_specs=placed,
        out_specs=P(None, None, None, "comp", ("elem", "rep")),
        check_vma=False,
    )
```

time: 417 us -> 114 us (0.27); the launches traced: 409 us -> 113 us
  starting transfers between devices: 92.2 us -> 0 us
  local copies, waits for them, and re-layouts: 148 us -> 65.8 us
  other arithmetic: 57.6 us -> 0 us
  Pallas kernels: 0 us -> 47.5 us
  waiting for transfers between devices: 40.2 us -> 0 us
  blocking collectives: 32.4 us -> 0 us
  matrix products: 31.4 us -> 0 us
  between operations: 6.91 us -> 0.01 us
    ppermute x26 -> x0, starting transfers between devices: 83.1 us -> none  [passed_along(): return lax.ppermute(x, axis, pairs)]
    add x4 -> x0, other arithmetic: 57.4 us -> none  [the longest x3 52.9 us: local_pass(): return field + jnp.where(node_iota == last_node, add_upper, 0.0)]
    broadcast_in_dim x61 -> x0, local copies, waits for them, and re-layouts: 51 us -> none  [the longest x54 32.5 us: add_region(): jnp.where(region_mask(field.shape, offset, block_grid), values, 0.0)]
    pallas_call x0 -> x1, Pallas kernels: none -> 47.5 us  [body(): pl.pallas_call(functools.partial(kernel, (n, half, tiles, table, rows, (c...]
    slice x18 -> x0, local copies, waits for them, and re-layouts: 44.9 us -> none  [the longest x7 18.2 us: take_region(): return field[nodes_key + elems_key]]
    all_to_all x2 -> x0, waiting for transfers between devices: 40.2 us -> none  [the longest x1 23.1 us: body(): lax.all_to_all(fluxes[2], 'comp', split_axis=3, concat_axis=0, tiled=True)]
    all_to_all x1 -> x0, blocking collectives: 32.4 us -> none  [body(): lax.all_to_all(fluxes[1], 'comp', split_axis=3, concat_axis=0, tiled=True)]
    dot_general x5 -> x0, matrix products: 31.4 us -> none  [the longest x1 13.5 us: body(): jnp.einsum('abcj,ij->abci', assembled, place_matrix, precision=exact_mode)]
  transfers between devices with their start and end apart: 28 -> 0, of which waited for: 2 -> 0; matrix products, arithmetic and copies ran while one was open for 12% -> 0% of each run, Pallas kernels for 0% -> 0%
where the time goes in v1:
time: 114 us; the launch traced here: 113 us
  local copies, waits for them, and re-layouts  65.8 us (58%)
  Pallas kernels  47.5 us (42%)
    pallas_call x1, Pallas kernels, body(): pl.pallas_call(functools.partial(kernel, (n, half, tiles, table, rows, (c...  47.5 us
    reshape x2, local copies, waits for them, and re-layouts, view(): x = x.reshape(lead + (n * n, 2, tiles, LANES))  34.3 us
    transpose x2, local copies, waits for them, and re-layouts, view(): x = jnp.swapaxes(x, -2, -3)  28 us
    reshape x1, local copies, waits for them, and re-layouts, body(): return result.reshape(n, n, n, 1, elems)  3.53 us

profile of v1, /device:TPU:1, one launch (start us, length us, event | category | flops | bytes accessed | tf_op | source)
XLA Modules:
  0.0 113.3 jit_solution(2753973374261890770)
XLA Ops:
  0.0 25.1 %reshape.17 = f32[3,3,5,100,2,3,128]{6,5,4,3,2,1,0:T(4,128)} reshape(f32[3,3,5,10,10,2,384]{6,5,4,3,2,1,0:T(2,128)} %param.5) | data formatting | bytes 27648000 | tf_op jit(solution)/shard_map/reshape | solution.py:436
  25.1 20.7 %copy.9 = f32[3,3,5,100,3,2,128]{6,5,4,3,2,1,0:T(2,128)} copy(f32[3,3,5,100,3,2,128]{6,4,5,3,2,1,0:T(4,128)} %bitcast.4) | data formatting | bytes 27648000 | tf_op jit(solution)/shard_map/transpose | solution.py:437
  45.9 9.1 %reshape.15 = f32[3,5,100,2,3,128]{5,4,3,2,1,0:T(4,128)} reshape(f32[3,5,10,10,2,384]{5,4,3,2,1,0:T(2,128)} %param.4) | data formatting | bytes 9216000 | tf_op jit(solution)/shard_map/reshape | solution.py:436
  55.0 7.3 %copy.8 = f32[3,5,100,3,2,128]{5,4,3,2,1,0:T(2,128)} copy(f32[3,5,100,3,2,128]{5,3,4,2,1,0:T(4,128)} %bitcast.6) | data formatting | bytes 9216000 | tf_op jit(solution)/shard_map/transpose | solution.py:437
  62.3 47.5 %shard_map.46 = f32[10,300,128]{2,1,0:T(8,128)} custom-call(s32[1,384]{1,0:T(1,128)} %place_ref.1, bf16[208,208]{1,0:T(8,128)(2,1)} %constant.10.kmat_ref, f32[3,5,600,128]{3,2,1,0:T(8,128)} %bitcast.7, f32[3,3,5,600,128]{4,3,2,1,0:T(8,128)} %bitcast.5), custom_call_target="tpu_custom_call" | custom-call | tf_op jit(solution)/shard_map/pallas_call | solution.py:445
  109.7 3.5 %reshape.20 = f32[10,10,10,1,384]{4,3,2,1,0:T(1,128)} reshape(f32[10,300,128]{2,1,0:T(8,128)} %shard_map.46) | data formatting | bytes 3072000 | tf_op jit(solution)/shard_map/reshape | solution.py:477

commit v2 on v1

--- a/solution.py
+++ b/solution.py
@@ -5,6 +5,7 @@
 import numpy as np
 from jax import lax
 from jax.experimental import pallas as pl
+from jax.experimental.layout import Layout, with_layout_constraint
 from jax.experimental.pallas import tpu as pltpu
 from jax.sharding import PartitionSpec as P
 
@@ -434,6 +435,9 @@
     def view(x):
         lead = x.shape[:-4]
         x = x.reshape(lead + (n * n, 2, tiles, LANES))
+        rank = len(lead)
+        order = tuple(range(rank + 1)) + (rank + 2, rank + 1, rank + 3)
+        x = with_layout_constraint(x, Layout(major_to_minor=order))
         x = jnp.swapaxes(x, -2, -3)
         return x.reshape(lead + (n * n * parts, LANES))
 

time: 114 us -> 51.2 us (0.45)
  local copies, waits for them, and re-layouts: 65.8 us -> 3.53 us
    reshape x2 -> x0, local copies, waits for them, and re-layouts: 34.3 us -> none  [view(): x = x.reshape(lead + (n * n, 2, tiles, LANES))]
    transpose x2 -> x0, local copies, waits for them, and re-layouts: 28 us -> none  [view(): x = jnp.swapaxes(x, -2, -3)]
where the time goes in v2:
time: 51.2 us; the launch traced here: 51 us
  Pallas kernels  47.5 us (93%)
  local copies, waits for them, and re-layouts  3.53 us (7%)
    pallas_call x1, Pallas kernels, body(): pl.pallas_call(functools.partial(kernel, (n, half, tiles, table, rows, (c...  47.5 us
    reshape x1, local copies, waits for them, and re-layouts, body(): return result.reshape(n, n, n, 1, elems)  3.53 us

profile of v2, /device:TPU:1, one launch (start us, length us, event | category | flops | bytes accessed | tf_op | source)
XLA Modules:
  0.0 51.0 jit_solution(7524221269083027459)
XLA Ops:
  0.0 47.5 %shard_map.46 = f32[10,300,128]{2,1,0:T(8,128)} custom-call(s32[1,384]{1,0:T(1,128)} %place_ref.1, bf16[208,208]{1,0:T(8,128)(2,1)} %constant.10.kmat_ref, f32[3,5,600,128]{3,2,1,0:T(8,128)} %bitcast.11, f32[3,3,5,600,128]{4,3,2,1,0:T(8,128)} %bitcast.10), custom_call_target="tpu_custom_call" | custom-call | tf_op jit(solution)/shard_map/pallas_call | solution.py:449
  47.5 3.5 %reshape.20 = f32[10,10,10,1,384]{4,3,2,1,0:T(1,128)} reshape(f32[10,300,128]{2,1,0:T(8,128)} %shard_map.46) | data formatting | bytes 3072000 | tf_op jit(solution)/shard_map/reshape | solution.py:481

commit v3 on v2

--- a/solution.py
+++ b/solution.py
@@ -108,7 +108,7 @@
 
 def kernel(sizes, place_ref, kmat_ref, vel_ref, geo_ref, out_ref,
            vel, geo, flux, stack, fbuf, sbuf, field, face, near, sel, selt, outb, inb,
-           load_sem, fsend, frecv, ssend, srecv, isend, irecv, nsend, nrecv):
+           ready, load_sem, fsend, frecv, ssend, srecv, isend, irecv, nsend, nrecv, out_sem):
     n, half, tiles, table, rows, counts = sizes
     m = rows.m
     parts = tiles * 2
@@ -236,7 +236,7 @@
         return carry
 
     lax.fori_loop(0, half, plane_terms, 0)
-    for k in range(1, half):
+    for k in range(1, half - 1):
         inner_copy(k, h).start()
 
     lanes = tiles * LANES
@@ -290,13 +290,6 @@
 
     lax.fori_loop(0, rows.plane_pad // 8, along_first, 0)
 
-    def arrive_faces(k, carry):
-        face_copy(k, other).wait_recv()
-        return carry
-
-    lax.fori_loop(0, half, arrive_faces, 0)
-    inner_copy(0, other).wait_recv()
-
     def add_faces(a, carry):
         for t in range(tiles):
             for start, count, at in (
@@ -308,8 +301,6 @@
                 field[a, t, at, :] = field[a, t, at, :] + sbuf[h, a, t, pl.ds(start, count), :]
         return carry
 
-    lax.fori_loop(0, n, add_faces, 0)
-
     def add_inner(a):
         for t in range(tiles):
             for b in range(m):
@@ -317,8 +308,11 @@
                 field[a, t, at, :] = (
                     field[a, t, at, :] + sbuf[h, a, t, pl.ds(rows.faces + b * m, m), :])
 
-    add_inner(0)
-    add_inner(n - 1)
+    face_copy(0, other).wait_recv()
+    inner_copy(0, other).wait_recv()
+    for a in (0, n - 1):
+        add_faces(a, 0)
+        add_inner(a)
 
     def take(d, side):
         node = side * (n - 1)
@@ -364,7 +358,22 @@
             send_sem=nsend.at[d, side], recv_sem=nrecv.at[d, side],
             device_id=neighbour(d, side), device_id_type=MESH)
 
+    def arrive_faces(k, carry):
+        face_copy(k, other).wait_recv()
+        add_faces(other * half + other * (half - 1) + k * (1 - 2 * other), 0)
+        return carry
+
+    def own_faces(k, carry):
+        add_faces(h * half + plane_at(k), 0)
+        return carry
+
+    def own_inner(k, carry):
+        add_inner(h * half + plane_at(k))
+        return carry
+
     for d in range(3):
+        if d == 1:
+            lax.fori_loop(1, half, arrive_faces, 0)
         for side in range(2):
             take(d, side)
         split = []
@@ -377,11 +386,17 @@
             @pl.when(has(d, side))
             def _():
                 step_copy(d, side).start()
+        if d == 2:
+            inner_copy(half - 1, h).start()
         totals = []
         for side in range(2):
             _, high, low = split[1 - side]
             totals.append(
                 split[side][0] + (dot(high, near[d, 1 - side]) + dot(low, near[d, 1 - side])))
+        if d == 0:
+            lax.fori_loop(1, half, own_faces, 0)
+        if d == 1:
+            lax.fori_loop(1, half, own_inner, 0)
         for side in range(2):
             @pl.when(has(d, side))
             def _():
@@ -393,24 +408,36 @@
         for side in range(2):
             give(d, side, totals[side] + pair_dot(inb[d, side], selt[d, side]))
 
-    def arrive_inner(k, carry):
+    def put_copy(p):
+        return pltpu.make_async_copy(ready.at[p], out_ref.at[p], out_sem.at[p])
+
+    def put(a):
+        first = (a % 2) * (rows.plane * tiles)
+        for t in range(tiles):
+            ready[a // 2, pl.ds(first + t, rows.plane, stride=tiles), :] = (
+                field[a, t, pl.ds(0, rows.plane), :])
+
+    put(0)
+    put(n - 1)
+
+    def put_own(k, carry):
+        put(h * half + plane_at(k))
+        return carry
+
+    lax.fori_loop(1, half, put_own, 0)
+    for p in range(half // 2):
+        put_copy(h * (n // 2 - half // 2) + p).start()
+    for k in range(1, half):
+        a = other * half + other * (half - 1) + k * (1 - 2 * other)
         inner_copy(k, other).wait_recv()
-        return carry
-
-    lax.fori_loop(1, half, arrive_inner, 0)
-
-    def inner_planes(a, carry):
         add_inner(a)
-        return carry
-
-    lax.fori_loop(1, n - 1, inner_planes, 0)
-
-    def put(a, carry):
-        for t in range(tiles):
-            out_ref[a, pl.ds(t, rows.plane, stride=tiles), :] = field[a, t, pl.ds(0, rows.plane), :]
-        return carry
-
-    lax.fori_loop(0, n, put, 0)
+        put(a)
+        if k % 2 == 1:
+            put_copy(a // 2).start()
+    if half % 2 == 1:
+        put_copy(half // 2).start()
+    for p in range(n // 2):
+        put_copy(p).wait()
 
     for k in range(half):
         flux_copy(k, h).wait_send()
@@ -448,14 +475,14 @@
     dma = pltpu.SemaphoreType.DMA
     result = pl.pallas_call(
         functools.partial(kernel, (n, half, tiles, table, rows, (comp_count, rep_count))),
-        out_shape=jax.ShapeDtypeStruct((n, n * n * tiles, LANES), f32),
+        out_shape=jax.ShapeDtypeStruct((n // 2, 2 * n * n * tiles, LANES), f32),
         in_specs=[
             pl.BlockSpec(memory_space=pltpu.VMEM),
             pl.BlockSpec(memory_space=pltpu.VMEM),
             pl.BlockSpec(memory_space=pl.ANY),
             pl.BlockSpec(memory_space=pl.ANY),
         ],
-        out_specs=pl.BlockSpec(memory_space=pltpu.VMEM),
+        out_specs=pl.BlockSpec(memory_space=pl.ANY),
         scratch_shapes=[
             pltpu.VMEM((3, half, long, LANES), f32),
             pltpu.VMEM((3, 3, half, long, LANES), f32),
@@ -470,14 +497,17 @@
             pltpu.VMEM((3, 2, LANES, elems), bf16),
             pltpu.VMEM((3, 2, deep, LANES), f32),
             pltpu.VMEM((3, 2, deep, LANES), f32),
+            pltpu.VMEM((n // 2, 2 * n * n * tiles, LANES), f32),
             dma((3, half)),
             dma((half,)), dma((half,)), dma((half,)), dma((half,)), dma((half,)), dma((half,)),
-            dma((3, 2)), dma((3, 2)),
+            dma((3, 2)), dma((3, 2)), dma((n // 2,)),
         ],
         compiler_params=pltpu.CompilerParams(
             collective_id=0, has_side_effects=True, vmem_limit_bytes=60 * 1024 * 1024
         ),
     )(element_place, plane_matrix(table, rows), view(velocity), view(geometry))
+    result = jnp.swapaxes(result.reshape(n, n, n, tiles, 1, LANES), 3, 4)
+    result = with_layout_constraint(result, Layout(major_to_minor=(0, 1, 2, 4, 3, 5)))
     return result.reshape(n, n, n, 1, elems)
 
 

time: 51.2 us -> 47.6 us (0.930); the launches traced: 51 us -> 46.7 us
  Pallas kernels: 47.5 us -> 43.1 us
    pallas_call x1, Pallas kernels: 47.5 us -> 43.1 us  [body(): pl.pallas_call(functools.partial(kernel, (n, half, tiles, table, rows, (c...]
    unnamed x0 -> x1, local copies, waits for them, and re-layouts: none -> 3.58 us
    reshape x1 -> x0, local copies, waits for them, and re-layouts: 3.53 us -> none  [body(): return result.reshape(n, n, n, 1, elems)]
where the time goes in v3:
time: 47.6 us; the launch traced here: 46.7 us
  Pallas kernels  43.1 us (91%)
  local copies, waits for them, and re-layouts  3.58 us (8%)
    pallas_call x1, Pallas kernels, body(): pl.pallas_call(functools.partial(kernel, (n, half, tiles, table, rows, (c...  43.1 us
    unnamed x1, local copies, waits for them, and re-layouts  3.58 us

profile of v3, /device:TPU:1, one launch (start us, length us, event | category | flops | bytes accessed | tf_op | source)
XLA Modules:
  0.0 46.7 jit_solution(9052943303585950578)
XLA Ops:
  0.0 43.1 %shard_map.46 = f32[5,600,128]{2,1,0:T(8,128)} custom-call(s32[1,384]{1,0:T(1,128)} %place_ref.1, bf16[208,208]{1,0:T(8,128)(2,1)} %constant.10.kmat_ref, f32[3,5,600,128]{3,2,1,0:T(8,128)} %bitcast.15, f32[3,3,5,600,128]{4,3,2,1,0:T(8,128)} %bitcast.13), custom_call_target="tpu_custom_call" | custom-call | tf_op jit(solution)/shard_map/pallas_call | solution.py:476
  43.1 3.6 %copy.7 = f32[10,10,10,1,384]{4,3,2,1,0:T(1,128)} copy(f32[10,10,10,1,384]{4,3,2,1,0:T(1,128)} %bitcast.14) | data formatting | bytes 3072000
